TPU v7x, 1024 devices: a whole 8x8x8 slice. The times are simulated.
1024 devices in a mesh: rows: 32 (over y_hi, x), cols: 4 (over y_lo, core), reps: 8 (over z).
Axes of the slice: x: 8, y: 8 (y_hi: 4, y_lo: 2; y = y_hi * 2 + y_lo), z: 8, core: 2. Of those that a mesh axis runs over, the one named last changes fastest.
Arguments:
- features: bfloat16 [32768, 512], P('rows', 'cols'), may hold values from -6 to 6
- tiles: bfloat16 [65536, 128, 128], P(('rows', 'reps')), may hold values from -0.1875 to 0.1875
- tile_cols: int32 [256, 256], P(('rows', 'reps')), may hold values from 0 to 255, as said below
- tile_ptr: int32 [256, 33], P(('rows', 'reps')), may hold values from 0 to 256, as said below
Outputs:
- aggregated: bfloat16 [32768, 512], P(('rows', 'reps'), 'cols')
Inputs may be any that keep to these rules, and one draw needn't show every extreme that they name: `tile_cols`: slot j of row g = b * 8 + q with key k (see steps) lies in section s = k // 8; its column tile is c * 8 + e with column block c = (b + q * 4 + s) mod 32 and 0 <= e < 8. Live slots name distinct tiles and are in order of key. Slots that are not live hold 0 and arbitrary tile values. `tile_ptr`: each row starts at 0 and never falls; its last entry, the live count, is at least 1 and equals 256 on some row of every draw; counts are skewed, most rows holding a quarter of 256 or less.
All inputs are finite; a program needn't handle non-finite values.
Results may differ from a plain program's by a relative error of at most 0.001.
Values may be sent and summed in bfloat16 or wider, within the bound.
No kernel may reach another device: no remote copies, remote signals or barrier semaphores. Data moves between devices by JAX's collectives and lax.ppermute only.
A program may use at most 64 MiB of HBM per device.

v0:
```python
import functools

import jax
import jax.numpy as jnp
from jax import lax
from jax.experimental import pallas as pl
from jax.experimental.pallas import tpu as pltpu
from jax.sharding import PartitionSpec as P


TB = 8
ACROSS = 1
CENTRE = 2
MIB = 1 << 20


def moved(block, sizes, source):
    rows, cols, reps = sizes

    def device(row, col, rep):
        return (row % rows * cols + col) * reps + rep % reps

    route = []
    for row in range(rows):
        for col in range(cols):
            for rep in range(reps):
                from_row, from_rep = source(row, col, rep)
                route.append((device(from_row, col, from_rep), device(row, col, rep)))
    return lax.ppermute(block, ("rows", "cols", "reps"), route)


def dense_kernel(sections, cols, ptr, tiles, dense, col_ids, pointers, table_sems, sem):
    size = tiles.shape[1]
    tables = [
        pltpu.make_async_copy(cols, col_ids, table_sems.at[0]),
        pltpu.make_async_copy(ptr, pointers, table_sems.at[1]),
    ]
    for table in tables:
        table.start()
    dense[...] = jnp.zeros(dense.shape, dense.dtype)
    for table in tables:
        table.wait()

    def tile_copy(slot, at, row, entry):
        where = dense.at[
            at, pl.ds(row * size, size), pl.ds(pl.multiple_of(entry * size, size), size)
        ]
        return pltpu.make_async_copy(tiles.at[slot], where, sem)

    for at, section in enumerate(sections):
        for row in range(TB):
            key = section * TB + row

            def send(slot, carry, at=at, row=row):
                tile_copy(slot, at, row, lax.rem(col_ids[0, slot], TB)).start()
                return carry

            lax.fori_loop(pointers[0, key], pointers[0, key + 1], send, 0)

    def arrive(slot, carry):
        tile_copy(0, 0, 0, 0).wait()
        return carry

    for section in sections:
        lax.fori_loop(pointers[0, section * TB], pointers[0, section * TB + TB], arrive, 0)


def dense_sections(sections, cols, ptr, tiles):
    size = tiles.shape[1]
    operands = [pltpu.with_memory_space_constraint(x, pltpu.HBM) for x in (cols, ptr, tiles)]
    return pl.pallas_call(
        functools.partial(dense_kernel, sections),
        out_shape=pltpu.VMEM((len(sections), TB * size, TB * size), tiles.dtype),
        in_specs=[pl.BlockSpec(memory_space=pl.ANY)] * 3,
        out_specs=pl.BlockSpec(memory_space=pltpu.VMEM),
        scratch_shapes=[
            pltpu.SMEM(cols.shape, cols.dtype),
            pltpu.SMEM(ptr.shape, ptr.dtype),
            pltpu.SemaphoreType.DMA((2,)),
            pltpu.SemaphoreType.DMA,
        ],
        compiler_params=pltpu.CompilerParams(vmem_limit_bytes=12 * MIB),
    )(*operands)


def product_kernel(count, chained, dense, *refs):
    feats = refs[:count]
    total = refs[-1]
    value = refs[count][...] if chained else None
    for at in range(count):
        part = jnp.dot(dense[at], feats[at][...], preferred_element_type=jnp.float32)
        value = part if value is None else value + part
    total[...] = value


def product_sum(dense, feats, start=None):
    operands = [dense, *feats] + ([] if start is None else [start])
    operands = [pltpu.with_memory_space_constraint(x, pltpu.VMEM) for x in operands]
    whole = pl.BlockSpec(memory_space=pltpu.VMEM)
    return pl.pallas_call(
        functools.partial(product_kernel, len(feats), start is not None),
        out_shape=pltpu.VMEM((dense.shape[1], feats[0].shape[1]), jnp.float32),
        in_specs=[whole] * len(operands),
        out_specs=whole,
        compiler_params=pltpu.CompilerParams(vmem_limit_bytes=16 * MIB),
    )(*operands)


def body(features, tiles, tile_cols, tile_ptr):
    size = tiles.shape[1]
    width = features.shape[1]
    sizes = [lax.axis_size(axis) for axis in ("rows", "cols", "reps")]
    rows, _, reps = sizes
    sections = rows // reps

    line = rows // 4

    def owner(section, crossing):
        def source(row, col, rep):
            across = col % 2 == crossing
            return row + sections * rep + section, rep ^ ACROSS if across else rep

        return source

    def neighbour(distance, turning):
        turn = distance * line // sections

        def source(row, col, rep):
            at = row % line + distance
            if col % 2 == turning and not 0 <= at < line:
                return row - row % line + at % line, rep + turn
            return row + distance, rep

        return source

    early, late = (CENTRE, 0), (CENTRE + 1, CENTRE - 1)
    dense_early = dense_sections(early, tile_cols, tile_ptr, tiles)
    dense_late = dense_sections(late, tile_cols, tile_ptr, tiles)
    centre = moved(features, sizes, owner(CENTRE, 1))
    first = moved(features, sizes, owner(0, 0))
    after = moved(centre, sizes, neighbour(1, 0))
    before = moved(centre, sizes, neighbour(-1, 1))
    partial = product_sum(dense_early, (centre, first))
    partial = product_sum(dense_late, (after, before), partial)
    blocks = partial.reshape(reps, size, width)
    arrived = lax.all_to_all(blocks, "reps", split_axis=0, concat_axis=0, tiled=True)
    return arrived.sum(axis=0).astype(jnp.bfloat16)


def solution(mesh):
    placed = (
        P("rows", "cols"),
        P(("rows", "reps"), None, None),
        P(("rows", "reps"), None),
        P(("rows", "reps"), None),
    )
    return jax.shard_map(
        body, mesh=mesh, in_specs=placed, out_specs=P(("rows", "reps"), "cols"), check_vma=False
    )
```

profile of v0, /device:TPU:100, one launch (start us, length us, event | category | flops | bytes accessed | tf_op | source)
XLA Modules:
  0.0 80.7 jit_solution(2879369121472736285)
XLA Ops:
  0.0 2.4 %collective-permute-start = (bf16[1024,128]{1,0:T(8,128)(2,1)}, bf16[1024,128]{1,0:T(8,128)(2,1)S(1)}, u32[]{:S(2)}, u32[]{:S(2)}) collective-permute-start(bf16[1024,128]{1,0:T(8,128)(2,1)} %param.4), channel_id=1, source_target_pairs={{64,0},{193,1},{322,2},{451,3},{580,4},{709,5},{838,6},{967,7},{73... | collective-permute-start | bytes 786440 | tf_op jit(solution)/shard_map/ppermute | solution.py:29
  2.4 9.5 %collective-permute-start.3 = (bf16[1024,128]{1,0:T(8,128)(2,1)}, bf16[1024,128]{1,0:T(8,128)(2,1)S(1)}, u32[]{:S(2)}, u32[]{:S(2)}) collective-permute-start(bf16[1024,128]{1,0:T(8,128)(2,1)} %param.4), channel_id=1, source_target_pairs={{1,0},{128,1},{259,2},{386,3},{517,4},{644,5},{775,6},{902,7},{8,8... | collective-permute-start | bytes 786440 | tf_op jit(solution)/shard_map/ppermute | solution.py:29
  12.0 1.4 %collective-permute-done.refs_0_ = bf16[1024,128]{1,0:T(8,128)(2,1)S(1)} collective-permute-done((bf16[1024,128]{1,0:T(8,128)(2,1)}, bf16[1024,128]{1,0:T(8,128)(2,1)S(1)}, u32[]{:S(2)}, u32[]{:S(2)}) %collective-permute-start) | collective-permute-done | bytes 262176 | tf_op jit(solution)/shard_map/ppermute | solution.py:29
  13.4 2.0 %collective-permute-start.2 = (bf16[1024,128]{1,0:T(8,128)(2,1)S(1)}, bf16[1024,128]{1,0:T(8,128)(2,1)S(1)}, u32[]{:S(2)}, u32[]{:S(2)}) collective-permute-start(bf16[1024,128]{1,0:T(8,128)(2,1)S(1)} %collective-permute-done.refs_0_), channel_id=1, source_target_pairs={{992,0},{993,1},{994,2},{995,3},{996,4},{997,5},{998,6},{999,7},{2... | collective-permute-start | bytes 786440 | tf_op jit(solution)/shard_map/ppermute | solution.py:29
  15.4 3.8 %collective-permute-start.1 = (bf16[1024,128]{1,0:T(8,128)(2,1)S(1)}, bf16[1024,128]{1,0:T(8,128)(2,1)S(1)}, u32[]{:S(2)}, u32[]{:S(2)}) collective-permute-start(bf16[1024,128]{1,0:T(8,128)(2,1)S(1)} %collective-permute-done.refs_0_), channel_id=1, source_target_pairs={{32,0},{33,1},{34,2},{35,3},{36,4},{37,5},{38,6},{39,7},{40,8},{41... | collective-permute-start | bytes 786440 | tf_op jit(solution)/shard_map/ppermute | solution.py:29
  19.2 2.4 %shard_map.47.dense = bf16[2,1024,1024]{2,1,0:T(8,128)(2,1)S(1)} custom-call(s32[1,256]{1,0:T(1,128)} %cols.3, s32[1,33]{1,0:T(1,128)} %ptr.3, bf16[256,128,128]{2,1,0:T(8,128)(2,1)} %tiles.3), custom_call_target="tpu_custom_call" | custom-call | tf_op jit(solution)/shard_map/pallas_call | solution.py:71
  21.6 2.5 %shard_map.46.dense = bf16[2,1024,1024]{2,1,0:T(8,128)(2,1)S(1)} custom-call(s32[1,256]{1,0:T(1,128)} %cols.3, s32[1,33]{1,0:T(1,128)} %ptr.3, bf16[256,128,128]{2,1,0:T(8,128)(2,1)} %tiles.3), custom_call_target="tpu_custom_call" | custom-call | tf_op jit(solution)/shard_map/pallas_call | solution.py:71
  24.1 0.0 collective-permute-done.3.refs_1_
  24.1 1.2 %shard_map.48.refs_2_ = f32[1024,128]{1,0:T(8,128)S(1)} custom-call(bf16[2,1024,1024]{2,1,0:T(8,128)(2,1)S(1)} %shard_map.47.dense, bf16[1024,128]{1,0:T(8,128)(2,1)S(1)} %collective-permute-done.refs_0_, bf16[1024,128]{1,0:T(8,128)(2,1)S(1)} %collective-permute-done.3.refs_1_), custom_call_target="tpu_custom_call" | custom-call | tf_op jit(solution)/shard_map/pallas_call | solution.py:100
  25.3 0.2 collective-permute-done.2.refs_1_
  25.5 0.0 collective-permute-done.1.refs_0_
  25.5 1.2 %shard_map.49 = f32[1024,128]{1,0:T(8,128)S(1)} custom-call(bf16[2,1024,1024]{2,1,0:T(8,128)(2,1)S(1)} %shard_map.46.dense, bf16[1024,128]{1,0:T(8,128)(2,1)S(1)} %collective-permute-done.1.refs_0_, bf16[1024,128]{1,0:T(8,128)(2,1)S(1)} %collective-permute-done.2.refs_1_, f32[1024,128]{1,0:T(8,128)S(1)} %shard_map.48.refs_2_), custom_call_target="tpu_custom_call" | custom-call | tf_op jit(solution)/shard_map/pallas_call | solution.py:100
  26.7 53.4 %all_to_all.5 = f32[8,128,128]{2,1,0:T(8,128)S(1)} all-to-all(f32[8,128,128]{2,1,0:T(8,128)S(1)} %bitcast.1), channel_id=1, replica_groups=mesh['rows'=32,'cols'=4,'reps'=8] {'reps'}, dimensions={0} | all-to-all | bytes 1048576 | tf_op jit(solution)/shard_map/all_to_all | solution.py:146
  80.1 0.6 reduce_sum.9
Async XLA Ops:
  0.0 13.4 %collective-permute-start = (bf16[1024,128]{1,0:T(8,128)(2,1)}, bf16[1024,128]{1,0:T(8,128)(2,1)S(1)}, u32[]{:S(2)}, u32[]{:S(2)}) collective-permute-start(bf16[1024,128]{1,0:T(8,128)(2,1)} %param.4), channel_id=1, source_target_pairs={{64,0},{193,1},{322,2},{451,3},{580,4},{709,5},{838,6},{967,7},{73... | collective-permute-start | bytes 786440 | tf_op jit(solution)/shard_map/ppermute | solution.py:29
  2.4 21.7 %collective-permute-start.3 = (bf16[1024,128]{1,0:T(8,128)(2,1)}, bf16[1024,128]{1,0:T(8,128)(2,1)S(1)}, u32[]{:S(2)}, u32[]{:S(2)}) collective-permute-start(bf16[1024,128]{1,0:T(8,128)(2,1)} %param.4), channel_id=1, source_target_pairs={{1,0},{128,1},{259,2},{386,3},{517,4},{644,5},{775,6},{902,7},{8,8... | collective-permute-start | bytes 786440 | tf_op jit(solution)/shard_map/ppermute | solution.py:29
  13.4 12.1 %collective-permute-start.2 = (bf16[1024,128]{1,0:T(8,128)(2,1)S(1)}, bf16[1024,128]{1,0:T(8,128)(2,1)S(1)}, u32[]{:S(2)}, u32[]{:S(2)}) collective-permute-start(bf16[1024,128]{1,0:T(8,128)(2,1)S(1)} %collective-permute-done.refs_0_), channel_id=1, source_target_pairs={{992,0},{993,1},{994,2},{995,3},{996,4},{997,5},{998,6},{999,7},{2... | collective-permute-start | bytes 786440 | tf_op jit(solution)/shard_map/ppermute | solution.py:29
  15.4 10.1 %collective-permute-start.1 = (bf16[1024,128]{1,0:T(8,128)(2,1)S(1)}, bf16[1024,128]{1,0:T(8,128)(2,1)S(1)}, u32[]{:S(2)}, u32[]{:S(2)}) collective-permute-start(bf16[1024,128]{1,0:T(8,128)(2,1)S(1)} %collective-permute-done.refs_0_), channel_id=1, source_target_pairs={{32,0},{33,1},{34,2},{35,3},{36,4},{37,5},{38,6},{39,7},{40,8},{41... | collective-permute-start | bytes 786440 | tf_op jit(solution)/shard_map/ppermute | solution.py:29
where the time goes:
time: 81.3 us; the launch traced here: 80.7 us
  blocking collectives  53.4 us (66%)
  starting transfers between devices  17.8 us (22%)
  Pallas kernels  7.31 us (9%)
  waiting for transfers between devices  1.58 us (2%)
    all_to_all x1, blocking collectives, body(): lax.all_to_all(blocks, 'reps', split_axis=0, concat_axis=0, tiled=True)  53.4 us
    ppermute x4, starting transfers between devices, moved(): return lax.ppermute(block, ('rows', 'cols', 'reps'), route)  17.8 us
    pallas_call x2, Pallas kernels, dense_sections(): pl.pallas_call(functools.partial(dense_kernel, sections), out_shape=pltpu...  4.82 us
    pallas_call x2, Pallas kernels, product_sum(): pl.pallas_call(functools.partial(product_kernel, len(feats), start is not...  2.49 us
  transfers between devices with their start and end apart: 4, of which 2 were waited for; matrix products, arithmetic and copies ran while one was open for 0% of the time, Pallas kernels for 8%

commit v1 on v0

--- a/solution.py
+++ b/solution.py
@@ -9,7 +9,8 @@
 
 
 TB = 8
-ACROSS = 1
+NEAR_PLANE = 1
+FAR_PLANE = 5
 CENTRE = 2
 MIB = 1 << 20
 
@@ -115,10 +116,10 @@
 
     line = rows // 4
 
-    def owner(section, crossing):
+    def owner(section, crossing, plane):
         def source(row, col, rep):
             across = col % 2 == crossing
-            return row + sections * rep + section, rep ^ ACROSS if across else rep
+            return row + sections * rep + section, rep ^ plane if across else rep
 
         return source
 
@@ -136,8 +137,8 @@
     early, late = (CENTRE, 0), (CENTRE + 1, CENTRE - 1)
     dense_early = dense_sections(early, tile_cols, tile_ptr, tiles)
     dense_late = dense_sections(late, tile_cols, tile_ptr, tiles)
-    centre = moved(features, sizes, owner(CENTRE, 1))
-    first = moved(features, sizes, owner(0, 0))
+    centre = moved(features, sizes, owner(CENTRE, 1, NEAR_PLANE))
+    first = moved(features, sizes, owner(0, 0, FAR_PLANE))
     after = moved(centre, sizes, neighbour(1, 0))
     before = moved(centre, sizes, neighbour(-1, 1))
     partial = product_sum(dense_early, (centre, first))

time: 81.3 us -> 76.2 us (0.937)
  the two profiles are of different devices: /device:TPU:100 before, /device:TPU:7 now
where the time goes in v1:
time: 76.2 us; the launch traced here: 75.6 us
  blocking collectives  45.1 us (59%)
  starting transfers between devices  18.3 us (24%)
  Pallas kernels  6.6 us (9%)
  waiting for transfers between devices  4.9 us (6%)
    all_to_all x1, blocking collectives, body(): lax.all_to_all(blocks, 'reps', split_axis=0, concat_axis=0, tiled=True)  45.1 us
    ppermute x4, starting transfers between devices, moved(): return lax.ppermute(block, ('rows', 'cols', 'reps'), route)  18.3 us
    ppermute x4, waiting for transfers between devices, moved(): return lax.ppermute(block, ('rows', 'cols', 'reps'), route)  4.9 us
    pallas_call x2, Pallas kernels, dense_sections(): pl.pallas_call(functools.partial(dense_kernel, sections), out_shape=pltpu...  4.11 us
    pallas_call x2, Pallas kernels, product_sum(): pl.pallas_call(functools.partial(product_kernel, len(feats), start is not...  2.49 us
  transfers between devices with their start and end apart: 4, of which 1 were waited for; matrix products, arithmetic and copies ran while one was open for 0% of the time, Pallas kernels for 7%

profile of v1, /device:TPU:7, one launch (start us, length us, event | category | flops | bytes accessed | tf_op | source)
XLA Modules:
  0.0 75.6 jit_solution(10910598889196764033)
XLA Ops:
  0.0 11.4 %collective-permute-start = (bf16[1024,128]{1,0:T(8,128)(2,1)}, bf16[1024,128]{1,0:T(8,128)(2,1)S(1)}, u32[]{:S(2)}, u32[]{:S(2)}) collective-permute-start(bf16[1024,128]{1,0:T(8,128)(2,1)} %param.4), channel_id=1, source_target_pairs={{64,0},{193,1},{322,2},{451,3},{580,4},{709,5},{838,6},{967,7},{73... | collective-permute-start | bytes 786440 | tf_op jit(solution)/shard_map/ppermute | solution.py:30
  11.4 1.6 %collective-permute-start.3 = (bf16[1024,128]{1,0:T(8,128)(2,1)}, bf16[1024,128]{1,0:T(8,128)(2,1)S(1)}, u32[]{:S(2)}, u32[]{:S(2)}) collective-permute-start(bf16[1024,128]{1,0:T(8,128)(2,1)} %param.4), channel_id=1, source_target_pairs={{5,0},{132,1},{263,2},{390,3},{513,4},{640,5},{771,6},{898,7},{8,8... | collective-permute-start | bytes 786440 | tf_op jit(solution)/shard_map/ppermute | solution.py:30
  13.1 4.9 %collective-permute-done.refs_0_ = bf16[1024,128]{1,0:T(8,128)(2,1)S(1)} collective-permute-done((bf16[1024,128]{1,0:T(8,128)(2,1)}, bf16[1024,128]{1,0:T(8,128)(2,1)S(1)}, u32[]{:S(2)}, u32[]{:S(2)}) %collective-permute-start) | collective-permute-done | bytes 262176 | tf_op jit(solution)/shard_map/ppermute | solution.py:30
  17.9 1.9 %collective-permute-start.2 = (bf16[1024,128]{1,0:T(8,128)(2,1)S(1)}, bf16[1024,128]{1,0:T(8,128)(2,1)S(1)}, u32[]{:S(2)}, u32[]{:S(2)}) collective-permute-start(bf16[1024,128]{1,0:T(8,128)(2,1)S(1)} %collective-permute-done.refs_0_), channel_id=1, source_target_pairs={{992,0},{993,1},{994,2},{995,3},{996,4},{997,5},{998,6},{999,7},{2... | collective-permute-start | bytes 786440 | tf_op jit(solution)/shard_map/ppermute | solution.py:30
  19.9 3.4 %collective-permute-start.1 = (bf16[1024,128]{1,0:T(8,128)(2,1)S(1)}, bf16[1024,128]{1,0:T(8,128)(2,1)S(1)}, u32[]{:S(2)}, u32[]{:S(2)}) collective-permute-start(bf16[1024,128]{1,0:T(8,128)(2,1)S(1)} %collective-permute-done.refs_0_), channel_id=1, source_target_pairs={{32,0},{33,1},{34,2},{35,3},{36,4},{37,5},{38,6},{39,7},{40,8},{41... | collective-permute-start | bytes 786440 | tf_op jit(solution)/shard_map/ppermute | solution.py:30
  23.2 2.0 %shard_map.47.dense = bf16[2,1024,1024]{2,1,0:T(8,128)(2,1)S(1)} custom-call(s32[1,256]{1,0:T(1,128)} %cols.3, s32[1,33]{1,0:T(1,128)} %ptr.3, bf16[256,128,128]{2,1,0:T(8,128)(2,1)} %tiles.3), custom_call_target="tpu_custom_call" | custom-call | tf_op jit(solution)/shard_map/pallas_call | solution.py:72
  25.3 2.1 %shard_map.46.dense = bf16[2,1024,1024]{2,1,0:T(8,128)(2,1)S(1)} custom-call(s32[1,256]{1,0:T(1,128)} %cols.3, s32[1,33]{1,0:T(1,128)} %ptr.3, bf16[256,128,128]{2,1,0:T(8,128)(2,1)} %tiles.3), custom_call_target="tpu_custom_call" | custom-call | tf_op jit(solution)/shard_map/pallas_call | solution.py:72
  27.4 0.0 collective-permute-done.3.refs_1_
  27.4 1.2 %shard_map.48.refs_2_ = f32[1024,128]{1,0:T(8,128)S(1)} custom-call(bf16[2,1024,1024]{2,1,0:T(8,128)(2,1)S(1)} %shard_map.47.dense, bf16[1024,128]{1,0:T(8,128)(2,1)S(1)} %collective-permute-done.refs_0_, bf16[1024,128]{1,0:T(8,128)(2,1)S(1)} %collective-permute-done.3.refs_1_), custom_call_target="tpu_custom_call" | custom-call | tf_op jit(solution)/shard_map/pallas_call | solution.py:101
  28.6 0.0 collective-permute-done.2.refs_1_
  28.6 0.0 collective-permute-done.1.refs_0_
  28.6 1.2 %shard_map.49 = f32[1024,128]{1,0:T(8,128)S(1)} custom-call(bf16[2,1024,1024]{2,1,0:T(8,128)(2,1)S(1)} %shard_map.46.dense, bf16[1024,128]{1,0:T(8,128)(2,1)S(1)} %collective-permute-done.1.refs_0_, bf16[1024,128]{1,0:T(8,128)(2,1)S(1)} %collective-permute-done.2.refs_1_, f32[1024,128]{1,0:T(8,128)S(1)} %shard_map.48.refs_2_), custom_call_target="tpu_custom_call" | custom-call | tf_op jit(solution)/shard_map/pallas_call | solution.py:101
  29.9 45.1 %all_to_all.5 = f32[8,128,128]{2,1,0:T(8,128)S(1)} all-to-all(f32[8,128,128]{2,1,0:T(8,128)S(1)} %bitcast.1), channel_id=1, replica_groups=mesh['rows'=32,'cols'=4,'reps'=8] {'reps'}, dimensions={0} | all-to-all | bytes 1048576 | tf_op jit(solution)/shard_map/all_to_all | solution.py:147
  75.0 0.6 reduce_sum.9
Async XLA Ops:
  0.0 17.9 %collective-permute-start = (bf16[1024,128]{1,0:T(8,128)(2,1)}, bf16[1024,128]{1,0:T(8,128)(2,1)S(1)}, u32[]{:S(2)}, u32[]{:S(2)}) collective-permute-start(bf16[1024,128]{1,0:T(8,128)(2,1)} %param.4), channel_id=1, source_target_pairs={{64,0},{193,1},{322,2},{451,3},{580,4},{709,5},{838,6},{967,7},{73... | collective-permute-start | bytes 786440 | tf_op jit(solution)/shard_map/ppermute | solution.py:30
  11.4 15.9 %collective-permute-start.3 = (bf16[1024,128]{1,0:T(8,128)(2,1)}, bf16[1024,128]{1,0:T(8,128)(2,1)S(1)}, u32[]{:S(2)}, u32[]{:S(2)}) collective-permute-start(bf16[1024,128]{1,0:T(8,128)(2,1)} %param.4), channel_id=1, source_target_pairs={{5,0},{132,1},{263,2},{390,3},{513,4},{640,5},{771,6},{898,7},{8,8... | collective-permute-start | bytes 786440 | tf_op jit(solution)/shard_map/ppermute | solution.py:30
  17.9 10.7 %collective-permute-start.2 = (bf16[1024,128]{1,0:T(8,128)(2,1)S(1)}, bf16[1024,128]{1,0:T(8,128)(2,1)S(1)}, u32[]{:S(2)}, u32[]{:S(2)}) collective-permute-start(bf16[1024,128]{1,0:T(8,128)(2,1)S(1)} %collective-permute-done.refs_0_), channel_id=1, source_target_pairs={{992,0},{993,1},{994,2},{995,3},{996,4},{997,5},{998,6},{999,7},{2... | collective-permute-start | bytes 786440 | tf_op jit(solution)/shard_map/ppermute | solution.py:30
  19.9 8.8 %collective-permute-start.1 = (bf16[1024,128]{1,0:T(8,128)(2,1)S(1)}, bf16[1024,128]{1,0:T(8,128)(2,1)S(1)}, u32[]{:S(2)}, u32[]{:S(2)}) collective-permute-start(bf16[1024,128]{1,0:T(8,128)(2,1)S(1)} %collective-permute-done.refs_0_), channel_id=1, source_target_pairs={{32,0},{33,1},{34,2},{35,3},{36,4},{37,5},{38,6},{39,7},{40,8},{41... | collective-permute-start | bytes 786440 | tf_op jit(solution)/shard_map/ppermute | solution.py:30

commit v2 on v1

--- a/solution.py
+++ b/solution.py
@@ -84,22 +84,22 @@
     )(*operands)
 
 
-def product_kernel(count, chained, dense, *refs):
+def product_kernel(offset, count, chained, dense, *refs):
     feats = refs[:count]
     total = refs[-1]
     value = refs[count][...] if chained else None
     for at in range(count):
-        part = jnp.dot(dense[at], feats[at][...], preferred_element_type=jnp.float32)
+        part = jnp.dot(dense[offset + at], feats[at][...], preferred_element_type=jnp.float32)
         value = part if value is None else value + part
     total[...] = value
 
 
-def product_sum(dense, feats, start=None):
+def product_sum(dense, feats, start=None, offset=0):
     operands = [dense, *feats] + ([] if start is None else [start])
     operands = [pltpu.with_memory_space_constraint(x, pltpu.VMEM) for x in operands]
     whole = pl.BlockSpec(memory_space=pltpu.VMEM)
     return pl.pallas_call(
-        functools.partial(product_kernel, len(feats), start is not None),
+        functools.partial(product_kernel, offset, len(feats), start is not None),
         out_shape=pltpu.VMEM((dense.shape[1], feats[0].shape[1]), jnp.float32),
         in_specs=[whole] * len(operands),
         out_specs=whole,
@@ -142,7 +142,8 @@
     after = moved(centre, sizes, neighbour(1, 0))
     before = moved(centre, sizes, neighbour(-1, 1))
     partial = product_sum(dense_early, (centre, first))
-    partial = product_sum(dense_late, (after, before), partial)
+    partial = product_sum(dense_late, (before,), partial, 1)
+    partial = product_sum(dense_late, (after,), partial)
     blocks = partial.reshape(reps, size, width)
     arrived = lax.all_to_all(blocks, "reps", split_axis=0, concat_axis=0, tiled=True)
     return arrived.sum(axis=0).astype(jnp.bfloat16)

time: 76.2 us -> 75.8 us (level)
  the two profiles are of different devices: /device:TPU:7 before, /device:TPU:102 now
where the time goes in v2:
time: 75.8 us; the launch traced here: 75.1 us
  blocking collectives  34 us (45%)
  starting transfers between devices  31.1 us (41%)
  Pallas kernels  7.47 us (10%)
  waiting for transfers between devices  1.81 us (2%)
    all_to_all x1, blocking collectives, body(): lax.all_to_all(blocks, 'reps', split_axis=0, concat_axis=0, tiled=True)  34 us
    ppermute x4, starting transfers between devices, moved(): return lax.ppermute(block, ('rows', 'cols', 'reps'), route)  31.1 us
    pallas_call x2, Pallas kernels, dense_sections(): pl.pallas_call(functools.partial(dense_kernel, sections), out_shape=pltpu...  4.82 us
    pallas_call x3, Pallas kernels, product_sum(): pl.pallas_call(functools.partial(product_kernel, offset, len(feats), star...  2.66 us
    ppermute x4, waiting for transfers between devices, moved(): return lax.ppermute(block, ('rows', 'cols', 'reps'), route)  1.81 us
  transfers between devices with their start and end apart: 4, of which 1 were waited for; matrix products, arithmetic and copies ran while one was open for 0% of the time, Pallas kernels for 9%

profile of v2, /device:TPU:102, one launch (start us, length us, event | category | flops | bytes accessed | tf_op | source)
XLA Modules:
  0.0 75.1 jit_solution(130368405950245042)
XLA Ops:
  0.0 2.4 %collective-permute-start = (bf16[1024,128]{1,0:T(8,128)(2,1)}, bf16[1024,128]{1,0:T(8,128)(2,1)S(1)}, u32[]{:S(2)}, u32[]{:S(2)}) collective-permute-start(bf16[1024,128]{1,0:T(8,128)(2,1)} %param.4), channel_id=1, source_target_pairs={{64,0},{193,1},{322,2},{451,3},{580,4},{709,5},{838,6},{967,7},{73... | collective-permute-start | bytes 786440 | tf_op jit(solution)/shard_map/ppermute | solution.py:30
  2.4 22.8 %collective-permute-start.3 = (bf16[1024,128]{1,0:T(8,128)(2,1)}, bf16[1024,128]{1,0:T(8,128)(2,1)S(1)}, u32[]{:S(2)}, u32[]{:S(2)}) collective-permute-start(bf16[1024,128]{1,0:T(8,128)(2,1)} %param.4), channel_id=1, source_target_pairs={{5,0},{132,1},{263,2},{390,3},{513,4},{640,5},{771,6},{898,7},{8,8... | collective-permute-start | bytes 786440 | tf_op jit(solution)/shard_map/ppermute | solution.py:30
  25.3 0.0 collective-permute-done.refs_0_
  25.3 3.4 %collective-permute-start.2 = (bf16[1024,128]{1,0:T(8,128)(2,1)S(1)}, bf16[1024,128]{1,0:T(8,128)(2,1)S(1)}, u32[]{:S(2)}, u32[]{:S(2)}) collective-permute-start(bf16[1024,128]{1,0:T(8,128)(2,1)S(1)} %collective-permute-done.refs_0_), channel_id=1, source_target_pairs={{992,0},{993,1},{994,2},{995,3},{996,4},{997,5},{998,6},{999,7},{2... | collective-permute-start | bytes 786440 | tf_op jit(solution)/shard_map/ppermute | solution.py:30
  28.7 2.4 %collective-permute-start.1 = (bf16[1024,128]{1,0:T(8,128)(2,1)S(1)}, bf16[1024,128]{1,0:T(8,128)(2,1)S(1)}, u32[]{:S(2)}, u32[]{:S(2)}) collective-permute-start(bf16[1024,128]{1,0:T(8,128)(2,1)S(1)} %collective-permute-done.refs_0_), channel_id=1, source_target_pairs={{32,0},{33,1},{34,2},{35,3},{36,4},{37,5},{38,6},{39,7},{40,8},{41... | collective-permute-start | bytes 786440 | tf_op jit(solution)/shard_map/ppermute | solution.py:30
  31.1 2.5 %shard_map.47.dense = bf16[2,1024,1024]{2,1,0:T(8,128)(2,1)S(1)} custom-call(s32[1,256]{1,0:T(1,128)} %cols.3, s32[1,33]{1,0:T(1,128)} %ptr.3, bf16[256,128,128]{2,1,0:T(8,128)(2,1)} %tiles.3), custom_call_target="tpu_custom_call" | custom-call | tf_op jit(solution)/shard_map/pallas_call | solution.py:72
  33.6 2.3 %shard_map.46.dense = bf16[2,1024,1024]{2,1,0:T(8,128)(2,1)S(1)} custom-call(s32[1,256]{1,0:T(1,128)} %cols.3, s32[1,33]{1,0:T(1,128)} %ptr.3, bf16[256,128,128]{2,1,0:T(8,128)(2,1)} %tiles.3), custom_call_target="tpu_custom_call" | custom-call | tf_op jit(solution)/shard_map/pallas_call | solution.py:72
  36.0 0.0 collective-permute-done.3.refs_1_
  36.0 1.2 %shard_map.48.refs_1_ = f32[1024,128]{1,0:T(8,128)S(1)} custom-call(bf16[2,1024,1024]{2,1,0:T(8,128)(2,1)S(1)} %shard_map.47.dense, bf16[1024,128]{1,0:T(8,128)(2,1)S(1)} %collective-permute-done.refs_0_, bf16[1024,128]{1,0:T(8,128)(2,1)S(1)} %collective-permute-done.3.refs_1_), custom_call_target="tpu_custom_call" | custom-call | tf_op jit(solution)/shard_map/pallas_call | solution.py:101
  37.2 0.0 collective-permute-done.2.refs_0_
  37.2 0.7 shard_map.49.refs_1_
  37.9 1.8 %collective-permute-done.1.refs_0_ = bf16[1024,128]{1,0:T(8,128)(2,1)S(1)} collective-permute-done((bf16[1024,128]{1,0:T(8,128)(2,1)S(1)}, bf16[1024,128]{1,0:T(8,128)(2,1)S(1)}, u32[]{:S(2)}, u32[]{:S(2)}) %collective-permute-start.1) | collective-permute-done | bytes 262176 | tf_op jit(solution)/shard_map/ppermute | solution.py:30
  39.7 0.7 shard_map.50
  40.5 34.0 %all_to_all.5 = f32[8,128,128]{2,1,0:T(8,128)S(1)} all-to-all(f32[8,128,128]{2,1,0:T(8,128)S(1)} %bitcast.1), channel_id=1, replica_groups=mesh['rows'=32,'cols'=4,'reps'=8] {'reps'}, dimensions={0} | all-to-all | bytes 1048576 | tf_op jit(solution)/shard_map/all_to_all | solution.py:148
  74.5 0.6 reduce_sum.9
Async XLA Ops:
  0.0 25.3 %collective-permute-start = (bf16[1024,128]{1,0:T(8,128)(2,1)}, bf16[1024,128]{1,0:T(8,128)(2,1)S(1)}, u32[]{:S(2)}, u32[]{:S(2)}) collective-permute-start(bf16[1024,128]{1,0:T(8,128)(2,1)} %param.4), channel_id=1, source_target_pairs={{64,0},{193,1},{322,2},{451,3},{580,4},{709,5},{838,6},{967,7},{73... | collective-permute-start | bytes 786440 | tf_op jit(solution)/shard_map/ppermute | solution.py:30
  2.4 33.5 %collective-permute-start.3 = (bf16[1024,128]{1,0:T(8,128)(2,1)}, bf16[1024,128]{1,0:T(8,128)(2,1)S(1)}, u32[]{:S(2)}, u32[]{:S(2)}) collective-permute-start(bf16[1024,128]{1,0:T(8,128)(2,1)} %param.4), channel_id=1, source_target_pairs={{5,0},{132,1},{263,2},{390,3},{513,4},{640,5},{771,6},{898,7},{8,8... | collective-permute-start | bytes 786440 | tf_op jit(solution)/shard_map/ppermute | solution.py:30
  25.3 12.0 %collective-permute-start.2 = (bf16[1024,128]{1,0:T(8,128)(2,1)S(1)}, bf16[1024,128]{1,0:T(8,128)(2,1)S(1)}, u32[]{:S(2)}, u32[]{:S(2)}) collective-permute-start(bf16[1024,128]{1,0:T(8,128)(2,1)S(1)} %collective-permute-done.refs_0_), channel_id=1, source_target_pairs={{992,0},{993,1},{994,2},{995,3},{996,4},{997,5},{998,6},{999,7},{2... | collective-permute-start | bytes 786440 | tf_op jit(solution)/shard_map/ppermute | solution.py:30
  28.7 11.1 %collective-permute-start.1 = (bf16[1024,128]{1,0:T(8,128)(2,1)S(1)}, bf16[1024,128]{1,0:T(8,128)(2,1)S(1)}, u32[]{:S(2)}, u32[]{:S(2)}) collective-permute-start(bf16[1024,128]{1,0:T(8,128)(2,1)S(1)} %collective-permute-done.refs_0_), channel_id=1, source_target_pairs={{32,0},{33,1},{34,2},{35,3},{36,4},{37,5},{38,6},{39,7},{40,8},{41... | collective-permute-start | bytes 786440 | tf_op jit(solution)/shard_map/ppermute | solution.py:30
